TPU v7x, 32 devices: a whole 2x2x4 slice. The times are simulated.
32 devices in a mesh: gx: 4 (over x, core), gy: 4 (over z), gz: 2 (over y).
Axes of the slice: x: 2, y: 2, z: 4, core: 2. Of those that a mesh axis runs over, the one named last changes fastest.
Arguments:
- amplitudes: bfloat16 [2, 16384, 2048], P(None, ('gx', 'gy', 'gz')), may hold values from -6 to 6
- pauli_x: int32 [200], replicated, may hold values from 0 to 2047, as said below
- pauli_z: int32 [200], replicated, may hold values from 0 to 2047
- pauli_phase: int32 [200], replicated, may hold values from 0 to 3
Outputs:
- density_real: float32 [2048, 2048], P(('gx', 'gy', 'gz'))
- density_imag: float32 [2048, 2048], P(('gx', 'gy', 'gz'))
- expectations: float32 [2, 200], replicated
Inputs may be any that keep to these rules, and one draw needn't show every extreme that they name: Bit q of the mask acts on kept qubit q (the bit of weight 2^q of the last index); pauli_x and pauli_z of a term are never both zero.
All inputs are finite; a program needn't handle non-finite values.
Results may differ from a plain program's by a relative error of at most 0.0003.
Values sent between devices are 32-bit elements; how exact they have to be, the bound alone decides.
A program may use at most 192 MiB of HBM per device.

v0:
```python
import functools

import jax
import jax.numpy as jnp
from jax import lax
from jax.experimental import pallas as pl
from jax.experimental.pallas import tpu as pltpu
from jax.sharding import PartitionSpec as P

AXES = ("gx", "gy", "gz")
LANES = 128
MESH = pl.DeviceIdType.MESH


def log2(value):
    return value.bit_length() - 1


def flat_index(sizes):
    return (lax.axis_index("gx") * sizes[1] + lax.axis_index("gy")) * sizes[2] + lax.axis_index("gz")


def coords(flat, sizes):
    return (flat // (sizes[1] * sizes[2]), (flat // sizes[2]) % sizes[1], flat % sizes[2])


def flip(bit, by):
    return bit + by - 2 * bit * by


def stage_order(sizes):
    zs = log2(sizes[2])
    ys = log2(sizes[1])
    xs = log2(sizes[0])
    rest_x = [zs + ys + t for t in range(xs - 1, 0, -1)]
    rest_y = [zs + t for t in range(ys)]
    rest_z = list(range(zs - 1, -1, -1))
    order = [zs + ys] + rest_x + rest_y[:1] + rest_z + rest_y[1:]
    trade = order.index(rest_z[0]) if rest_x and rest_z else 1
    return order, trade


def parity_sign(masked):
    shift = 16
    while shift >= 1:
        masked = jnp.bitwise_xor(masked, jnp.right_shift(masked, shift))
        shift //= 2
    return (1 - 2 * jnp.bitwise_and(masked, 1)).astype(jnp.float32)


def gram_kernel(
    sizes, total_cols, amp, px, pz, phase, kept, mirrored, expect,
    ext, part, land, turned, came, outbox, inbox, load_sem, send_sem, recv_sem, msend, mrecv, esend, erecv,
):
    n = sizes[0] * sizes[1] * sizes[2]
    nbits = log2(n)
    depth = amp.shape[1]
    order = amp.shape[2]
    own = order // n
    block = max(own, LANES)
    q = block // own
    blocks = order // block
    width = (blocks // 2 + 1) * block
    me = flat_index(sizes)
    bits = [(me // (1 << p)) % 2 for p in range(nbits)]
    stages, trade = stage_order(sizes)
    half = bits[stages[0]]

    def loads():
        out = []
        for part_index in range(2):
            rows = pl.ds(part_index * depth, depth)
            out.append(pltpu.make_async_copy(amp.at[part_index], ext.at[rows, pl.ds(0, order)], load_sem.at[2 * part_index]))
            out.append(
                pltpu.make_async_copy(
                    amp.at[part_index, :, pl.ds(0, width - block)],
                    ext.at[rows, pl.ds(order, width - block)],
                    load_sem.at[2 * part_index + 1],
                )
            )
        return out

    for copy in loads():
        copy.start()

    def flips_of(v):
        by_stage = [(v >> (nbits - 1 - s)) & 1 for s in range(nbits)]
        flips = [0] * nbits
        for s, p in enumerate(stages):
            flips[p] = by_stage[s]
        if by_stage[1] != by_stage[trade]:
            flips[stages[1]] = by_stage[1] * (1 - half) + by_stage[trade] * half
            flips[stages[trade]] = by_stage[trade] * (1 - half) + by_stage[1] * half
        return flips

    def place(flips):
        return sum((1 << p) * flip(bits[p], flips[p]) for p in range(nbits))

    def name(flips):
        return sum((1 << p) * flips[p] for p in range(nbits))

    def message(where, ident, target, c):
        cols = pl.ds(c * width, width)
        return pltpu.make_async_remote_copy(
            src_ref=part.at[where, :, cols],
            dst_ref=land.at[ident, :, cols],
            send_sem=send_sem.at[2 * ident + c],
            recv_sem=recv_sem.at[2 * ident + c],
            device_id=coords(target, sizes),
            device_id_type=MESH,
        )

    partner = [place(flips_of(1 << (nbits - 1 - s))) for s in range(nbits)]
    lowbits = log2(q)
    high = [p for p in stages[-1:] + stages[1:-1] if p >= lowbits]

    def row_block(u):
        flips = [0] * nbits
        flips[stages[0]] = 1 - u % 2
        for j, p in enumerate(high):
            flips[p] = 1 - (u // (1 << (len(high) - j))) % 2
        return flips

    for copy in loads():
        copy.wait()

    def add_in(where, names, c):
        cols = slice(c * width, (c + 1) * width)
        for ident in names:
            message(where, ident, partner[0], c).wait_recv()
        for r in range(0, own, 8):
            rows = pl.ds(r, 8)
            total = part[where, rows, cols]
            for ident in names:
                total = total + land[ident, rows, cols]
            part[where, rows, cols] = total

    def with_low(flips, g):
        return [(g >> p) & 1 if p < lowbits else flips[p] for p in range(nbits)]

    def second_stage(w):
        for g in range(q):
            flips = with_low(row_block(2 * w + 1), g)
            goes = flips[stages[1]] * (1 - half) + flips[stages[trade]] * half

            @pl.when(goes == 1)
            def _():
                where, ident = place(flips), name(flips)
                for c in range(2):
                    add_in(where, [ident + (1 << stages[0])], c)
                    message(where, ident, partner[1], c).start()

    def compute(u, _):
        @pl.when(u % 2 == 1)
        def _():
            for g in range(q):
                flips = with_low(row_block(u - 1), g)
                for c in range(2):
                    message(place(flips), name(flips), partner[0], c).start()

        @pl.when((u % 2 == 1) & (u >= 5))
        def _():
            second_stage(u // 2 - 2)

        flips = row_block(u)
        first = sum((1 << p) * flip(bits[p], flips[p]) for p in range(lowbits, nbits))
        start = pl.multiple_of(first * own, block)
        lhs = ext[:, pl.ds(start, block)]
        crossed = jnp.concatenate([lhs[depth:], -lhs[:depth]], 0)
        both = jnp.concatenate([lhs, crossed], 1)
        rhs = ext[:, pl.ds(start, width)]
        rows = lax.dot_general(both, rhs, (((0,), (0,)), ((), ())), preferred_element_type=jnp.float32)
        for sub in range(q):
            part[first + sub, :, 0:width] = rows[sub * own : (sub + 1) * own]
            part[first + sub, :, width : 2 * width] = rows[block + sub * own : block + (sub + 1) * own]
        return 0

    lax.fori_loop(0, blocks, compute, 0)

    for w in range(max(blocks // 2 - 2, 0), blocks // 2):
        second_stage(w)

    def gather_in(v, upto, c):
        where = place(flips_of(v))
        add_in(where, [name(flips_of(v | (1 << (nbits - 1 - t)))) for t in range(upto)], c)
        return where

    later = 1 << (nbits - 2)
    for v in sorted(range(1, later), key=lambda v: (v % 2 == 0, -v)):
        s = nbits - v.bit_length()
        for c in range(2):
            where = gather_in(v, s, c)
            message(where, name(flips_of(v)), partner[s], c).start()

    for c in range(2):
        gather_in(0, nbits, c)
    for r in range(0, own, 8):
        rows = pl.ds(r, 8)
        kept[rows, :] = part[me, rows, :] / total_cols

    mine = me // q
    sub_me = me % q

    def mirror(k, sub):
        target = ((mine + k) % blocks) * q + sub
        return pltpu.make_async_remote_copy(
            src_ref=turned.at[k - 1, pl.ds(sub * own, own)],
            dst_ref=came.at[(k - 1) * q + sub_me],
            send_sem=msend.at[(k - 1) * q + sub],
            recv_sem=mrecv.at[(k - 1) * q + sub_me],
            device_id=coords(target, sizes),
            device_id_type=MESH,
        )

    for k in range(1, blocks // 2):
        cols = kept[:, k * block : (k + 1) * block]
        more = kept[:, width + k * block : width + (k + 1) * block]
        turned[k - 1] = jnp.concatenate([cols, more], 0).T
    for k in range(1, blocks // 2):
        for sub in range(q):
            mirror(k, sub).start()
    terms = px.shape[1]
    base = me * own
    ids = base + lax.broadcasted_iota(jnp.int32, (own, terms), 0)
    signs = parity_sign(jnp.bitwise_and(ids, pz[...]))
    paired = parity_sign(jnp.bitwise_and(px[...], pz[...]))
    wanted = jnp.bitwise_xor(px[...], base)
    row = lax.broadcasted_iota(jnp.int32, (own, block), 0)
    lane = lax.broadcasted_iota(jnp.int32, (own, block), 1)
    lane_terms = lax.broadcasted_iota(jnp.int32, (block, terms), 0)

    def picked(first, k):
        values = kept[:, first + k * block : first + (k + 1) * block]
        for p in range(log2(own)):
            step = 1 << p
            swapped = jnp.where(
                jnp.bitwise_and(lane, step) != 0,
                pltpu.roll(values, step, 1),
                pltpu.roll(values, block - step, 1),
            )
            values = jnp.where(jnp.bitwise_and(row, step) != 0, swapped, values)
        sums = lax.dot_general(
            values, signs, (((0,), (0,)), ((), ())), precision=lax.Precision.HIGHEST, preferred_element_type=jnp.float32
        )
        chosen = jnp.where(lane_terms + ((mine + k) % blocks) * block == wanted, sums, 0.0)
        return jnp.sum(chosen, axis=0, keepdims=True)

    def row_sums(first, sign):
        ends = picked(first, 0) + picked(first, blocks // 2)
        inner = jnp.zeros_like(ends)
        for k in range(1, blocks // 2):
            inner = inner + picked(first, k)
        return ends + inner * (1.0 + sign * paired)

    sum_real = row_sums(0, 1.0)
    sum_imag = row_sums(width, -1.0)
    turn = phase[...]
    phase_real = jnp.where(turn == 0, 1.0, jnp.where(turn == 2, -1.0, 0.0))
    phase_imag = jnp.where(turn == 1, 1.0, jnp.where(turn == 3, -1.0, 0.0))
    total = jnp.concatenate(
        [phase_real * sum_real - phase_imag * sum_imag, phase_real * sum_imag + phase_imag * sum_real], 0
    )
    here = coords(me, sizes)
    first_slot = 0
    for axis in range(3):
        size = sizes[axis]
        at = here[axis]
        outbox[axis] = total
        inbox[first_slot + at] = total
        copies = []
        for d in range(1, size):
            target = list(here)
            target[axis] = (at + d) % size
            copies.append(
                pltpu.make_async_remote_copy(
                    src_ref=outbox.at[axis],
                    dst_ref=inbox.at[first_slot + at],
                    send_sem=esend.at[first_slot + d],
                    recv_sem=erecv.at[first_slot + at],
                    device_id=tuple(target),
                    device_id_type=MESH,
                )
            )
        for copy in copies:
            copy.start()
        for d in range(1, size):
            source = first_slot + (at + d) % size
            pltpu.make_async_remote_copy(
                src_ref=outbox.at[axis],
                dst_ref=inbox.at[source],
                send_sem=esend.at[first_slot + d],
                recv_sem=erecv.at[source],
                device_id=tuple(target),
                device_id_type=MESH,
            ).wait()
        total = inbox[first_slot]
        for j in range(1, size):
            total = total + inbox[first_slot + j]
        first_slot += size
    expect[...] = total

    for k in range(1, blocks // 2):
        for sub in range(q):
            slot = (k - 1) * q + sub
            pltpu.make_async_remote_copy(
                src_ref=turned.at[k - 1, pl.ds(sub * own, own)],
                dst_ref=came.at[slot],
                send_sem=msend.at[slot],
                recv_sem=mrecv.at[slot],
                device_id=coords(((mine + k) % blocks) * q + sub, sizes),
                device_id_type=MESH,
            ).wait()
            mirrored[slot] = came[slot]

    def drain(ident, _):
        for c in range(2):
            message(0, ident, partner[0], c).wait_send()
        return 0

    lax.fori_loop(1, n, drain, 0)


def finish_kernel(sizes, kept, mirrored, real, imag):
    n = sizes[0] * sizes[1] * sizes[2]
    own, order = real.shape
    block = max(own, LANES)
    q = block // own
    blocks = order // block
    width = (blocks // 2 + 1) * block
    me = flat_index(sizes)
    mine = me // q

    def columns(k):
        return pl.ds(pl.multiple_of(((mine + k + blocks) % blocks) * block, block), block)

    for k in range(blocks // 2 + 1):
        real[:, columns(k)] = kept[:, k * block : (k + 1) * block]
        imag[:, columns(k)] = kept[:, width + k * block : width + (k + 1) * block]
    for k in range(1, blocks // 2):
        tiles = [mirrored[(k - 1) * q + sub] for sub in range(q)]
        real[:, columns(-k)] = jnp.concatenate([t[:, :own] for t in tiles], 1)
        imag[:, columns(-k)] = -jnp.concatenate([t[:, own:] for t in tiles], 1)


def on_device(sizes, amplitudes, pauli_x, pauli_z, pauli_phase):
    n = sizes[0] * sizes[1] * sizes[2]
    _, depth, order = amplitudes.shape
    own = order // n
    block = max(own, LANES)
    q = block // own
    blocks = order // block
    width = (blocks // 2 + 1) * block
    slots = (blocks // 2 - 1) * q
    vmem = pl.BlockSpec(memory_space=pltpu.VMEM)
    terms = pauli_x.shape[0]
    kept, mirrored, expect = pl.pallas_call(
        functools.partial(gram_kernel, sizes, float(depth * n)),
        out_shape=(
            jax.ShapeDtypeStruct((own, 2 * width), jnp.float32),
            jax.ShapeDtypeStruct((slots, own, 2 * own), jnp.float32),
            jax.ShapeDtypeStruct((2, terms), jnp.float32),
        ),
        in_specs=[pl.BlockSpec(memory_space=pl.ANY), vmem, vmem, vmem],
        out_specs=(vmem,) * 3,
        scratch_shapes=[
            pltpu.VMEM((2 * depth, order + width - block), jnp.bfloat16),
            pltpu.VMEM((n, own, 2 * width), jnp.float32),
            pltpu.VMEM((n, own, 2 * width), jnp.float32),
            pltpu.VMEM((blocks // 2 - 1, block, 2 * own), jnp.float32),
            pltpu.VMEM((slots, own, 2 * own), jnp.float32),
            pltpu.VMEM((3, 2, terms), jnp.float32),
            pltpu.VMEM((sum(sizes), 2, terms), jnp.float32),
            pltpu.SemaphoreType.DMA((4,)),
            pltpu.SemaphoreType.DMA((2 * n,)),
            pltpu.SemaphoreType.DMA((2 * n,)),
            pltpu.SemaphoreType.DMA((slots,)),
            pltpu.SemaphoreType.DMA((slots,)),
            pltpu.SemaphoreType.DMA((sum(sizes),)),
            pltpu.SemaphoreType.DMA((sum(sizes),)),
        ],
        compiler_params=pltpu.CompilerParams(has_side_effects=True, vmem_limit_bytes=60 << 20),
    )(amplitudes, pauli_x[None], pauli_z[None], pauli_phase[None])
    real, imag = pl.pallas_call(
        functools.partial(finish_kernel, sizes),
        out_shape=(
            jax.ShapeDtypeStruct((own, order), jnp.float32),
            jax.ShapeDtypeStruct((own, order), jnp.float32),
        ),
        in_specs=[vmem] * 2,
        out_specs=(vmem,) * 2,
    )(kept, mirrored)
    return real, imag, expect


def solution(mesh):
    sizes = tuple(mesh.shape[axis] for axis in AXES)
    return jax.shard_map(
        functools.partial(on_device, sizes),
        mesh=mesh,
        in_specs=(P(None, AXES, None), P(), P(), P()),
        out_specs=(P(AXES, None), P(AXES, None), P()),
        check_vma=False,
    )
```

profile of v0, /device:TPU:0, one launch (start us, length us, event | category | flops | bytes accessed | tf_op | source)
XLA Modules:
  0.0 118.4 jit_solution(14322758953226754787)
XLA Ops:
  0.6 114.2 %shard_map.67 = (f32[64,2304]{1,0:T(8,128)}, f32[14,64,128]{2,1,0:T(8,128)}, f32[2,200]{1,0:T(2,128)}) custom-call(bf16[2,512,2048]{2,1,0:T(8,128)(2,1)} %amp.1, s32[1,200]{1,0:T(1,128)} %bitcast.3, s32[1,200]{1,0:T(1,128)} %bitcast.4, s32[1,200]{1,0:T(1,128)} %bitcast.5), custom_call_target="tpu_custom_call" | custom-call | tf_op jit(solution)/shard_map/pallas_call | solution.py:356
  114.8 2.3 %shard_map.68 = (f32[64,2048]{1,0:T(8,128)}, f32[64,2048]{1,0:T(8,128)}) custom-call(f32[64,2304]{1,0:T(8,128)} %get-tuple-element.8.kept, f32[14,64,128]{2,1,0:T(8,128)} %get-tuple-element.9.mirrored), custom_call_target="tpu_custom_call" | custom-call | tf_op jit(solution)/shard_map/pallas_call | solution.py:383
  117.2 1.2 %copy.8 = f32[2,200]{1,0:T(2,128)} copy(f32[2,200]{1,0:T(2,128)} %get-tuple-element.18) | data formatting | bytes 3200
where the time goes:
time: 119 us; the launch traced here: 118 us
  Pallas kernels  117 us (98%)
  local copies, waits for them, and re-layouts  1.23 us (1%)
    pallas_call x1, Pallas kernels, on_device(): pl.pallas_call(functools.partial(gram_kernel, sizes, float(depth * n)), o...  114 us

commit v1 on v0

v1 whole, which is shorter than its diff:
```python
import functools

import jax
import jax.numpy as jnp
from jax import lax
from jax.experimental import pallas as pl
from jax.experimental.pallas import tpu as pltpu
from jax.sharding import PartitionSpec as P

AXES = ("gx", "gy", "gz")
LANES = 128
EARLY = 2
MESH = pl.DeviceIdType.MESH


def log2(value):
    return value.bit_length() - 1


def flat_index(sizes):
    return (lax.axis_index("gx") * sizes[1] + lax.axis_index("gy")) * sizes[2] + lax.axis_index("gz")


def coords(flat, sizes):
    return (flat // (sizes[1] * sizes[2]), (flat // sizes[2]) % sizes[1], flat % sizes[2])


def flip(bit, by):
    return bit + by - 2 * bit * by


def stage_order(sizes):
    zs = log2(sizes[2])
    ys = log2(sizes[1])
    xs = log2(sizes[0])
    rest_x = [zs + ys + t for t in range(xs - 1, 0, -1)]
    rest_y = [zs + t for t in range(ys)]
    rest_z = list(range(zs - 1, -1, -1))
    order = [zs + ys] + rest_x + rest_y[:1] + rest_z + rest_y[1:]
    trade = order.index(rest_z[0]) if rest_x and rest_z else 1
    return order, trade


def parity_sign(masked):
    shift = 16
    while shift >= 1:
        masked = jnp.bitwise_xor(masked, jnp.right_shift(masked, shift))
        shift //= 2
    return (1 - 2 * jnp.bitwise_and(masked, 1)).astype(jnp.float32)


def row_order(sizes, q):
    nbits = log2(sizes[0] * sizes[1] * sizes[2])
    stages, _ = stage_order(sizes)
    lowbits = log2(q)
    return [p for p in stages[2:3] + stages[4:] + stages[1:2] + stages[3:4] if lowbits <= p < nbits]


def early_items(sizes, q, lag):
    nbits = log2(sizes[0] * sizes[1] * sizes[2])
    stages, trade = stage_order(sizes)
    high = row_order(sizes, q)

    def pair_of(v, half):
        by_stage = [(v >> (nbits - 1 - s)) & 1 for s in range(nbits)]
        if half:
            by_stage[1], by_stage[trade] = by_stage[trade], by_stage[1]
        flips = {p: by_stage[s] for s, p in enumerate(stages)}
        w = 0
        for p in high:
            w = 2 * w + 1 - flips[p]
        return w

    out = []
    for v in range((1 << (nbits - 2)) - 1, (1 << (nbits - 3)) - 1, -1):
        waits = []
        for half in range(2):
            waits.append(2 * pair_of(v, half) + 1 + lag)
            waits.append(2 * pair_of(v | (1 << (nbits - 2)), half) + 1 + 2 * lag)
        out.append((max(waits), v))
    return sorted(out, key=lambda item: (item[0], -item[1]))


def gram_kernel(
    sizes, total_cols, early, amp, px, pz, phase, kept, mirrored, expect,
    ext, part, land, turned, came, spread, tally, outbox, inbox, load_sem, send_sem, recv_sem, msend, mrecv, esend, erecv,
):
    n = sizes[0] * sizes[1] * sizes[2]
    nbits = log2(n)
    depth = amp.shape[1]
    order = amp.shape[2]
    own = order // n
    block = max(own, LANES)
    q = block // own
    blocks = order // block
    width = (blocks // 2 + 1) * block
    slabs = part.shape[1]
    chunks = recv_sem.shape[0] // n
    group = slabs // chunks
    me = flat_index(sizes)
    bits = [(me // (1 << p)) % 2 for p in range(nbits)]
    stages, trade = stage_order(sizes)
    half = bits[stages[0]]
    lag = 4

    def loads():
        out = []
        for part_index in range(2):
            rows = pl.ds(part_index * depth, depth)
            out.append(pltpu.make_async_copy(amp.at[part_index], ext.at[rows, pl.ds(0, order)], load_sem.at[2 * part_index]))
            out.append(
                pltpu.make_async_copy(
                    amp.at[part_index, :, pl.ds(0, width - block)],
                    ext.at[rows, pl.ds(order, width - block)],
                    load_sem.at[2 * part_index + 1],
                )
            )
        return out

    for copy in loads():
        copy.start()

    def flips_of(v):
        by_stage = [(v >> (nbits - 1 - s)) & 1 for s in range(nbits)]
        flips = [0] * nbits
        for s, p in enumerate(stages):
            flips[p] = by_stage[s]
        flips[stages[1]] = by_stage[1] * (1 - half) + by_stage[trade] * half
        flips[stages[trade]] = by_stage[trade] * (1 - half) + by_stage[1] * half
        return flips

    def place(flips):
        return sum((1 << p) * flip(bits[p], flips[p]) for p in range(nbits))

    def name(flips):
        return sum((1 << p) * flips[p] for p in range(nbits))

    partner = [place(flips_of(1 << (nbits - 1 - s))) for s in range(nbits)]
    lowbits = log2(q)
    high = row_order(sizes, q)

    def message(where, ident, target, c):
        piece = pl.ds(c * group, group)
        return pltpu.make_async_remote_copy(
            src_ref=part.at[where, piece],
            dst_ref=land.at[ident, piece],
            send_sem=send_sem.at[ident],
            recv_sem=recv_sem.at[ident * chunks + c],
            device_id=coords(target, sizes),
            device_id_type=MESH,
        )

    def whole(where, ident):
        return pltpu.make_async_remote_copy(
            src_ref=part.at[where],
            dst_ref=land.at[ident],
            send_sem=send_sem.at[ident],
            recv_sem=recv_sem.at[ident * chunks],
            device_id=coords(partner[0], sizes),
            device_id_type=MESH,
        )

    def row_block(u):
        flips = [0] * nbits
        flips[stages[0]] = 1 - u % 2
        for j, p in enumerate(high):
            flips[p] = 1 - (u // (1 << (len(high) - j))) % 2
        return flips

    def with_low(flips, g):
        return [(g >> p) & 1 if p < lowbits else flips[p] for p in range(nbits)]

    def summed(where, names, slab, rows):
        total = part[where, slab, rows, :]
        for ident in names:
            total = total + land[ident, slab, rows, :]
        return total

    def second_stage(w, upto):
        for g in range(q):
            flips = with_low(row_block(2 * w + 1), g)
            goes = flips[stages[1]] * (1 - half) + flips[stages[trade]] * half

            @pl.when(goes == 1)
            def _():
                where, ident = place(flips), name(flips)
                whole(where, ident + (1 << stages[0])).wait_recv()
                for slab in range(slabs):
                    for r in range(0, own, 8):
                        rows = pl.ds(r, 8)
                        part[where, slab, rows, :] = summed(where, [ident + (1 << stages[0])], slab, rows)
                for c in range(upto):
                    message(where, ident, partner[1], c).start()

    def later_second(w, c):
        for g in range(q):
            flips = with_low(row_block(2 * w + 1), g)
            goes = flips[stages[1]] * (1 - half) + flips[stages[trade]] * half

            @pl.when(goes == 1)
            def _():
                message(place(flips), name(flips), partner[1], c).start()

    def arrive(v, upto, c, first):
        names = [name(flips_of(v | (1 << (nbits - 1 - t)))) for t in range(upto)]

        def core_to_core():
            whole(0, names[0]).wait_recv()

        if isinstance(first, bool):
            if first:
                core_to_core()
        else:
            pl.when(first)(core_to_core)
        for ident in names[1:]:
            message(0, ident, partner[0], c).wait_recv()
        return names

    def item(v, s, c, first):
        names = arrive(v, s, c, first)
        flips = flips_of(v)
        where = place(flips)
        for g in range(group):
            slab = c * group + g
            for r in range(0, own, 8):
                rows = pl.ds(r, 8)
                part[where, slab, rows, :] = summed(where, names, slab, rows)
        message(where, name(flips), partner[s], c).start()

    terms = px.shape[1]
    mine = me // q
    sub_me = me % q
    base = me * own

    for copy in loads():
        copy.wait()

    row_in = lax.broadcasted_iota(jnp.int32, (block, block), 0)
    lane_in = lax.broadcasted_iota(jnp.int32, (block, block), 1)
    seconds = early_items(sizes, q, lag)

    def compute(u, _):
        @pl.when(u % 2 == 1)
        def _():
            for g in range(q):
                flips = with_low(row_block(u - 1), g)
                whole(place(flips), name(flips)).start()

        @pl.when((u % 2 == 1) & (u >= 1 + lag))
        def _():
            second_stage((u - lag) // 2, early)

        for at in sorted({at for at, _ in seconds if at < blocks}):

            @pl.when(u == at)
            def _():
                for when, v in seconds:
                    if when == at:
                        item(v, 2, 0, True)

        flips = row_block(u)
        first = sum((1 << p) * flip(bits[p], flips[p]) for p in range(lowbits, nbits))
        start = pl.multiple_of(first * own, block)
        lhs = ext[:, pl.ds(start, block)]
        crossed = jnp.concatenate([lhs[depth:], -lhs[:depth]], 0)
        both = jnp.concatenate([lhs, crossed], 1)
        rhs = ext[:, pl.ds(start, width)]
        rows = lax.dot_general(both, rhs, (((0,), (0,)), ((), ())), preferred_element_type=jnp.float32)
        bound = jnp.where(first // q < blocks // 2, 0, -1)
        near = jnp.where(row_in - lane_in <= 0, rows[:block, :block], rows[block:, :block])
        far = jnp.where(row_in - lane_in <= bound, rows[:block, width - block :], rows[block:, width - block :])
        for sub in range(q):
            at = slice(sub * own, (sub + 1) * own)
            more = slice(block + sub * own, block + (sub + 1) * own)
            for k in range(1, slabs):
                cols = slice(k * block, (k + 1) * block)
                part[first + sub, k - 1, :, 0:block] = rows[at, cols]
                part[first + sub, k - 1, :, block : 2 * block] = rows[more, cols]
            part[first + sub, slabs - 1, :, 0:block] = near[at]
            part[first + sub, slabs - 1, :, block : 2 * block] = far[at]
        return 0

    lax.fori_loop(0, blocks, compute, 0)

    for w in range(max(blocks // 2 - lag // 2, 0), blocks // 2):
        second_stage(w, early)
    for at, v in seconds:
        if at >= blocks:
            item(v, 2, 0, True)

    def send_later(c, _):
        for w in range(blocks // 2):
            later_second(w, c)
        return 0

    lax.fori_loop(early, chunks, send_later, 0)

    turn = phase[...]
    paired = parity_sign(jnp.bitwise_and(px[...], pz[...]))
    wanted = jnp.bitwise_xor(px[...], base)
    lane_terms = lax.broadcasted_iota(jnp.int32, (block, terms), 0)
    row = lax.broadcasted_iota(jnp.int32, (own, block), 0)
    lane = lax.broadcasted_iota(jnp.int32, (own, block), 1)
    ids = base + lax.broadcasted_iota(jnp.int32, (own, terms), 0)
    signs = parity_sign(jnp.bitwise_and(ids, pz[...]))
    signs_real = jnp.where(paired > 0, signs, 0.0)
    signs_imag = jnp.where(paired > 0, 0.0, signs)
    spread[...] = jnp.concatenate([signs_real] * 3 + [signs_imag] * 3, 0).astype(jnp.bfloat16)
    tally[...] = jnp.zeros_like(tally)

    def swapped_rows(values):
        for p in range(log2(own)):
            step = 1 << p
            swapped = jnp.where(
                jnp.bitwise_and(lane, step) != 0,
                pltpu.roll(values, step, 1),
                pltpu.roll(values, block - step, 1),
            )
            values = jnp.where(jnp.bitwise_and(row, step) != 0, swapped, values)
        return values

    def in_three(values):
        high_part = values.astype(jnp.bfloat16)
        rest = values - high_part.astype(jnp.float32)
        middle = rest.astype(jnp.bfloat16)
        low = (rest - middle.astype(jnp.float32)).astype(jnp.bfloat16)
        return [high_part, middle, low]

    def pick(real_values, imag_values, k):
        stacked = jnp.concatenate(in_three(swapped_rows(real_values)) + in_three(swapped_rows(imag_values)), 0)
        sums = lax.dot_general(stacked, spread[...], (((0,), (0,)), ((), ())), preferred_element_type=jnp.float32)
        chosen = jnp.where(lane_terms + ((mine + k) % blocks) * block == wanted, sums, 0.0)
        tally[...] = tally[...] + jnp.sum(chosen, axis=0, keepdims=True)

    def mirror(k, sub, source, slot):
        return pltpu.make_async_remote_copy(
            src_ref=turned.at[source, pl.ds(sub * own, own)],
            dst_ref=came.at[slot * q + sub_me],
            send_sem=msend.at[slot * q + sub],
            recv_sem=mrecv.at[slot * q + sub_me],
            device_id=coords(((mine + k) % blocks) * q + sub, sizes),
            device_id_type=MESH,
        )

    def mirror_from(k, sub, slot):
        return pltpu.make_async_remote_copy(
            src_ref=turned.at[0, pl.ds(sub * own, own)],
            dst_ref=came.at[slot * q + sub],
            send_sem=msend.at[slot * q + sub],
            recv_sem=mrecv.at[slot * q + sub],
            device_id=coords(((mine + k) % blocks) * q + sub, sizes),
            device_id_type=MESH,
        )

    local_row = sub_me * own + row
    bound_me = jnp.where(mine < blocks // 2, 0, -1)

    def finish(c):
        names = arrive(0, nbits, c, c == 0)
        for g in range(group):
            slab = c * group + g
            for r in range(0, own, 8):
                rows = pl.ds(r, 8)
                kept[slab, rows, :] = summed(me, names, slab, rows) / total_cols
            turned[slab] = jnp.concatenate([kept[slab, :, :block], kept[slab, :, block:]], 0).T

            @pl.when(slab < slabs - 1)
            def _():
                for sub in range(q):
                    mirror(slab + 1, sub, slab, slab).start()
                pick(kept[slab, :, :block], kept[slab, :, block:], slab + 1)

        @pl.when(c == chunks - 1)
        def _():
            slab = slabs - 1
            for sub in range(q):
                mirror(slabs, sub, slab, slab).start()

                @pl.when(sub != sub_me)
                def _():
                    mirror(0, sub, slab, slabs).start()

                @pl.when(sub == sub_me)
                def _():
                    mirrored[slabs * q + sub] = turned[slab, sub * own : (sub + 1) * own]

            near = kept[slab, :, :block]
            upper = jnp.where(local_row < lane, near, jnp.where(local_row == lane, 0.5 * near, 0.0))
            pick(upper, jnp.where(local_row > lane, near, 0.0), 0)
            far = kept[slab, :, block:]
            holds = local_row - lane <= bound_me
            pick(jnp.where(holds, far, 0.0), jnp.where(holds, 0.0, far), slabs)

    last = nbits - 2

    def step(t, _):
        for s in range(2, nbits):
            c = t - (s - 2)
            if s == 2:
                first, live = False, c < chunks
            else:
                first, live = c == 0, (c >= 0) & (c < chunks)

            @pl.when(live)
            def _():
                for v in range((1 << (nbits - s)) - 1, (1 << (nbits - 1 - s)) - 1, -1):
                    item(v, s, c, first)

        @pl.when((t >= last) & (t - last < chunks))
        def _():
            finish(t - last)

        return 0

    lax.fori_loop(1, chunks + last, step, 0)

    sums = 2.0 * tally[...]
    sum_real = jnp.where(paired > 0, sums, 0.0)
    sum_imag = jnp.where(paired > 0, 0.0, sums)
    phase_real = jnp.where(turn == 0, 1.0, jnp.where(turn == 2, -1.0, 0.0))
    phase_imag = jnp.where(turn == 1, 1.0, jnp.where(turn == 3, -1.0, 0.0))
    total = jnp.concatenate(
        [phase_real * sum_real - phase_imag * sum_imag, phase_real * sum_imag + phase_imag * sum_real], 0
    )
    outbox[...] = total
    inbox[me] = total

    def share(d, to):
        return pltpu.make_async_remote_copy(
            src_ref=outbox,
            dst_ref=inbox.at[to],
            send_sem=esend.at[d],
            recv_sem=erecv.at[to],
            device_id=coords((me + d) % n, sizes),
            device_id_type=MESH,
        )

    def share_out(d, _):
        share(d, me).start()
        return 0

    lax.fori_loop(1, n, share_out, 0)

    for k in range(1, slabs + 1):
        for sub in range(q):
            slot = (k - 1) * q + sub
            mirror_from(k, sub, k - 1).wait()
            mirrored[slot] = came[slot]
    for sub in range(q):

        @pl.when(sub != sub_me)
        def _():
            mirror_from(0, sub, slabs).wait()
            mirrored[slabs * q + sub] = came[slabs * q + sub]

    def drain(ident, _):
        whole(0, ident).wait_send()
        return 0

    lax.fori_loop(1, n, drain, 0)

    def share_in(d, _):
        share(d, (me + d) % n).wait()
        return 0

    lax.fori_loop(1, n, share_in, 0)

    total = inbox[0]
    for j in range(1, n):
        total = total + inbox[j]
    expect[...] = total


def finish_kernel(sizes, kept, mirrored, expected, real, imag, expect):
    n = sizes[0] * sizes[1] * sizes[2]
    own, order = real.shape
    block = max(own, LANES)
    q = block // own
    blocks = order // block
    slabs = kept.shape[0]
    me = flat_index(sizes)
    mine = me // q
    sub_me = me % q

    def columns(k):
        return pl.ds(pl.multiple_of(((mine + k + blocks) % blocks) * block, block), block)

    def turned(slot, side):
        return jnp.concatenate([mirrored[slot * q + sub][:, side * own : (side + 1) * own] for sub in range(q)], 1)

    for k in range(1, slabs):
        real[:, columns(k)] = kept[k - 1, :, :block]
        imag[:, columns(k)] = kept[k - 1, :, block:]
        real[:, columns(-k)] = turned(k - 1, 0)
        imag[:, columns(-k)] = -turned(k - 1, 1)
    row = sub_me * own + lax.broadcasted_iota(jnp.int32, (own, block), 0)
    lane = lax.broadcasted_iota(jnp.int32, (own, block), 1)
    near, other = kept[slabs - 1, :, :block], turned(slabs, 0)
    real[:, columns(0)] = jnp.where(row <= lane, near, other)
    imag[:, columns(0)] = jnp.where(row > lane, near, jnp.where(row < lane, -other, 0.0))
    far, other = kept[slabs - 1, :, block:], turned(slabs - 1, 1)
    holds = row - lane <= jnp.where(mine < blocks // 2, 0, -1)
    real[:, columns(slabs)] = jnp.where(holds, far, other)
    imag[:, columns(slabs)] = jnp.where(holds, -other, far)
    expect[...] = expected[...]


def on_device(sizes, amplitudes, pauli_x, pauli_z, pauli_phase):
    n = sizes[0] * sizes[1] * sizes[2]
    _, depth, order = amplitudes.shape
    own = order // n
    block = max(own, LANES)
    q = block // own
    blocks = order // block
    slabs = blocks // 2
    group = min(slabs, max(1, LANES // (2 * own)))
    chunks = slabs // group
    width = (slabs + 1) * block
    slots = (slabs + 1) * q
    vmem = pl.BlockSpec(memory_space=pltpu.VMEM)
    terms = pauli_x.shape[0]
    kept, mirrored, expect = pl.pallas_call(
        functools.partial(gram_kernel, sizes, float(depth * n), min(EARLY, chunks)),
        out_shape=(
            jax.ShapeDtypeStruct((slabs, own, 2 * block), jnp.float32),
            jax.ShapeDtypeStruct((slots, own, 2 * own), jnp.float32),
            jax.ShapeDtypeStruct((2, terms), jnp.float32),
        ),
        in_specs=[pl.BlockSpec(memory_space=pl.ANY), vmem, vmem, vmem],
        out_specs=(vmem,) * 3,
        scratch_shapes=[
            pltpu.VMEM((2 * depth, order + width - block), jnp.bfloat16),
            pltpu.VMEM((n, slabs, own, 2 * block), jnp.float32),
            pltpu.VMEM((n, slabs, own, 2 * block), jnp.float32),
            pltpu.VMEM((slabs, block, 2 * own), jnp.float32),
            pltpu.VMEM((slots, own, 2 * own), jnp.float32),
            pltpu.VMEM((6 * own, terms), jnp.bfloat16),
            pltpu.VMEM((1, terms), jnp.float32),
            pltpu.VMEM((2, terms), jnp.float32),
            pltpu.VMEM((n, 2, terms), jnp.float32),
            pltpu.SemaphoreType.DMA((4,)),
            pltpu.SemaphoreType.DMA((n,)),
            pltpu.SemaphoreType.DMA((n * chunks,)),
            pltpu.SemaphoreType.DMA((slots,)),
            pltpu.SemaphoreType.DMA((slots,)),
            pltpu.SemaphoreType.DMA((n,)),
            pltpu.SemaphoreType.DMA((n,)),
        ],
        compiler_params=pltpu.CompilerParams(has_side_effects=True, vmem_limit_bytes=60 << 20),
    )(amplitudes, pauli_x[None], pauli_z[None], pauli_phase[None])
    real, imag, expect = pl.pallas_call(
        functools.partial(finish_kernel, sizes),
        out_shape=(
            jax.ShapeDtypeStruct((own, order), jnp.float32),
            jax.ShapeDtypeStruct((own, order), jnp.float32),
            jax.ShapeDtypeStruct((2, terms), jnp.float32),
        ),
        in_specs=[vmem] * 3,
        out_specs=(vmem,) * 3,
    )(kept, mirrored, expect)
    return real, imag, expect


def solution(mesh):
    sizes = tuple(mesh.shape[axis] for axis in AXES)
    return jax.shard_map(
        functools.partial(on_device, sizes),
        mesh=mesh,
        in_specs=(P(None, AXES, None), P(), P(), P()),
        out_specs=(P(AXES, None), P(AXES, None), P()),
        check_vma=False,
    )
```

time: 119 us -> 109 us (0.916)
  Pallas kernels: 117 us -> 108 us
  local copies, waits for them, and re-layouts: 1.23 us -> 0 us
    pallas_call x1, Pallas kernels: 114 us -> 106 us  [on_device(): pl.pallas_call(functools.partial(gram_kernel, sizes, float(depth * n), mi...]
    unnamed x1 -> x0, local copies, waits for them, and re-layouts: 1.23 us -> none
where the time goes in v1:
time: 109 us
  Pallas kernels  108 us (99%)
    pallas_call x1, Pallas kernels, on_device(): pl.pallas_call(functools.partial(gram_kernel, sizes, float(depth * n), mi...  106 us
    pallas_call x1, Pallas kernels, on_device(): pl.pallas_call(functools.partial(finish_kernel, sizes), out_shape=(jax.Sh...  2.39 us

profile of v1, /device:TPU:0, one launch (start us, length us, event | category | flops | bytes accessed | tf_op | source)
XLA Modules:
  0.0 109.0 jit_solution(7164675673218084950)
XLA Ops:
  0.6 106.0 %shard_map.67 = (f32[8,64,256]{2,1,0:T(8,128)}, f32[18,64,128]{2,1,0:T(8,128)}, f32[2,200]{1,0:T(2,128)}) custom-call(bf16[2,512,2048]{2,1,0:T(8,128)(2,1)} %amp.1, s32[1,200]{1,0:T(1,128)} %bitcast.3, s32[1,200]{1,0:T(1,128)} %bitcast.4, s32[1,200]{1,0:T(1,128)} %bitcast.5), custom_call_target="tpu_custom_call" | custom-call | tf_op jit(solution)/shard_map/pallas_call | solution.py:522
  106.6 2.4 %shard_map.68 = (f32[64,2048]{1,0:T(8,128)}, f32[64,2048]{1,0:T(8,128)}, f32[2,200]{1,0:T(2,128)}) custom-call(f32[8,64,256]{2,1,0:T(8,128)} %get-tuple-element.6.kept, f32[18,64,128]{2,1,0:T(8,128)} %get-tuple-element.7.mirrored, f32[2,200]{1,0:T(2,128)} %get-tuple-element.8.expected), custom_call_target="tpu_custom_call" | custom-call | tf_op jit(solution)/shard_map/pallas_call | solution.py:551

commit v2 on v1

--- a/solution.py
+++ b/solution.py
@@ -10,6 +10,7 @@
 AXES = ("gx", "gy", "gz")
 LANES = 128
 EARLY = 2
+VMEM_LIMIT = 60 << 20
 MESH = pl.DeviceIdType.MESH
 
 
@@ -56,7 +57,7 @@
     return [p for p in stages[2:3] + stages[4:] + stages[1:2] + stages[3:4] if lowbits <= p < nbits]
 
 
-def early_items(sizes, q, lag):
+def early_items(sizes, q, lag, flight):
     nbits = log2(sizes[0] * sizes[1] * sizes[2])
     stages, trade = stage_order(sizes)
     high = row_order(sizes, q)
@@ -76,7 +77,7 @@
         waits = []
         for half in range(2):
             waits.append(2 * pair_of(v, half) + 1 + lag)
-            waits.append(2 * pair_of(v | (1 << (nbits - 2)), half) + 1 + 2 * lag)
+            waits.append(2 * pair_of(v | (1 << (nbits - 2)), half) + 1 + lag + flight)
         out.append((max(waits), v))
     return sorted(out, key=lambda item: (item[0], -item[1]))
 
@@ -97,11 +98,14 @@
     slabs = part.shape[1]
     chunks = recv_sem.shape[0] // n
     group = slabs // chunks
+    passes = 2
+    per_pass = chunks // passes
+    part_slabs = slabs // passes
     me = flat_index(sizes)
     bits = [(me // (1 << p)) % 2 for p in range(nbits)]
     stages, trade = stage_order(sizes)
     half = bits[stages[0]]
-    lag = 4
+    lag, late_lag, flight = 4, blocks // 2, 6
 
     def loads():
         out = []
@@ -117,8 +121,6 @@
             )
         return out
 
-    for copy in loads():
-        copy.start()
 
     def flips_of(v):
         by_stage = [(v >> (nbits - 1 - s)) & 1 for s in range(nbits)]
@@ -136,6 +138,11 @@
         return sum((1 << p) * flips[p] for p in range(nbits))
 
     partner = [place(flips_of(1 << (nbits - 1 - s))) for s in range(nbits)]
+    barrier = pltpu.get_barrier_semaphore()
+    for other in partner:
+        pl.semaphore_signal(barrier, inc=1, device_id=coords(other, sizes), device_id_type=MESH)
+    for copy in loads():
+        copy.start()
     lowbits = log2(q)
     high = row_order(sizes, q)
 
@@ -150,12 +157,13 @@
             device_id_type=MESH,
         )
 
-    def whole(where, ident):
+    def across(where, ident, which):
+        piece = pl.ds(which * part_slabs, part_slabs)
         return pltpu.make_async_remote_copy(
-            src_ref=part.at[where],
-            dst_ref=land.at[ident],
+            src_ref=part.at[where, piece],
+            dst_ref=land.at[ident, piece],
             send_sem=send_sem.at[ident],
-            recv_sem=recv_sem.at[ident * chunks],
+            recv_sem=recv_sem.at[ident * chunks + which],
             device_id=coords(partner[0], sizes),
             device_id_type=MESH,
         )
@@ -176,7 +184,7 @@
             total = total + land[ident, slab, rows, :]
         return total
 
-    def second_stage(w, upto):
+    def second_stage(w, which, upto):
         for g in range(q):
             flips = with_low(row_block(2 * w + 1), g)
             goes = flips[stages[1]] * (1 - half) + flips[stages[trade]] * half
@@ -184,12 +192,12 @@
             @pl.when(goes == 1)
             def _():
                 where, ident = place(flips), name(flips)
-                whole(where, ident + (1 << stages[0])).wait_recv()
-                for slab in range(slabs):
+                across(where, ident + (1 << stages[0]), which).wait_recv()
+                for slab in range(which * part_slabs, (which + 1) * part_slabs):
                     for r in range(0, own, 8):
                         rows = pl.ds(r, 8)
                         part[where, slab, rows, :] = summed(where, [ident + (1 << stages[0])], slab, rows)
-                for c in range(upto):
+                for c in range(which * per_pass, which * per_pass + upto):
                     message(where, ident, partner[1], c).start()
 
     def later_second(w, c):
@@ -201,23 +209,19 @@
             def _():
                 message(place(flips), name(flips), partner[1], c).start()
 
-    def arrive(v, upto, c, first):
+    def arrive(v, upto, c):
         names = [name(flips_of(v | (1 << (nbits - 1 - t)))) for t in range(upto)]
 
-        def core_to_core():
-            whole(0, names[0]).wait_recv()
-
-        if isinstance(first, bool):
-            if first:
-                core_to_core()
-        else:
-            pl.when(first)(core_to_core)
+        @pl.when(c % per_pass == 0)
+        def _():
+            across(0, names[0], c // per_pass).wait_recv()
+
         for ident in names[1:]:
             message(0, ident, partner[0], c).wait_recv()
         return names
 
-    def item(v, s, c, first):
-        names = arrive(v, s, c, first)
+    def item(v, s, c):
+        names = arrive(v, s, c)
         flips = flips_of(v)
         where = place(flips)
         for g in range(group):
@@ -237,63 +241,101 @@
 
     row_in = lax.broadcasted_iota(jnp.int32, (block, block), 0)
     lane_in = lax.broadcasted_iota(jnp.int32, (block, block), 1)
-    seconds = early_items(sizes, q, lag)
-
-    def compute(u, _):
-        @pl.when(u % 2 == 1)
-        def _():
-            for g in range(q):
-                flips = with_low(row_block(u - 1), g)
-                whole(place(flips), name(flips)).start()
-
-        @pl.when((u % 2 == 1) & (u >= 1 + lag))
-        def _():
-            second_stage((u - lag) // 2, early)
-
-        for at in sorted({at for at, _ in seconds if at < blocks}):
-
-            @pl.when(u == at)
-            def _():
-                for when, v in seconds:
-                    if when == at:
-                        item(v, 2, 0, True)
-
+    seconds = early_items(sizes, q, lag, flight)
+
+    def gram(u, which):
         flips = row_block(u)
         first = sum((1 << p) * flip(bits[p], flips[p]) for p in range(lowbits, nbits))
         start = pl.multiple_of(first * own, block)
         lhs = ext[:, pl.ds(start, block)]
         crossed = jnp.concatenate([lhs[depth:], -lhs[:depth]], 0)
         both = jnp.concatenate([lhs, crossed], 1)
-        rhs = ext[:, pl.ds(start, width)]
-        rows = lax.dot_general(both, rhs, (((0,), (0,)), ((), ())), preferred_element_type=jnp.float32)
-        bound = jnp.where(first // q < blocks // 2, 0, -1)
-        near = jnp.where(row_in - lane_in <= 0, rows[:block, :block], rows[block:, :block])
-        far = jnp.where(row_in - lane_in <= bound, rows[:block, width - block :], rows[block:, width - block :])
+
+        def product(k, count):
+            rhs = ext[:, pl.ds(pl.multiple_of(start + k * block, block), count * block)]
+            return lax.dot_general(both, rhs, (((0,), (0,)), ((), ())), preferred_element_type=jnp.float32)
+
+        low = which * part_slabs
+        rows = product(low + 1, part_slabs)
+        closing = which == passes - 1
+        plain = part_slabs - 1 if closing else part_slabs
+        if closing:
+            here = product(0, 1)
+            far_cols = slice(plain * block, (plain + 1) * block)
+            bound = jnp.where(first // q < blocks // 2, 0, -1)
+            near = jnp.where(row_in - lane_in <= 0, here[:block], here[block:])
+            far = jnp.where(row_in - lane_in <= bound, rows[:block, far_cols], rows[block:, far_cols])
         for sub in range(q):
             at = slice(sub * own, (sub + 1) * own)
             more = slice(block + sub * own, block + (sub + 1) * own)
-            for k in range(1, slabs):
+            for k in range(plain):
                 cols = slice(k * block, (k + 1) * block)
-                part[first + sub, k - 1, :, 0:block] = rows[at, cols]
-                part[first + sub, k - 1, :, block : 2 * block] = rows[more, cols]
-            part[first + sub, slabs - 1, :, 0:block] = near[at]
-            part[first + sub, slabs - 1, :, block : 2 * block] = far[at]
+                part[first + sub, low + k, :, 0:block] = rows[at, cols]
+                part[first + sub, low + k, :, block : 2 * block] = rows[more, cols]
+            if closing:
+                part[first + sub, slabs - 1, :, 0:block] = near[at]
+                part[first + sub, slabs - 1, :, block : 2 * block] = far[at]
+
+    def hand_over(u, which):
+        for g in range(q):
+            flips = with_low(row_block(u), g)
+            across(place(flips), name(flips), which).start()
+
+    def compute(u, _):
+        @pl.when(u == 1)
+        def _():
+            pl.semaphore_wait(barrier, nbits)
+
+        @pl.when(u % 2 == 1)
+        def _():
+            hand_over(u - 1, 0)
+
+        @pl.when((u % 2 == 1) & (u >= 1 + lag))
+        def _():
+            second_stage((u - lag) // 2, 0, early)
+
+        for at in sorted({at for at, _ in seconds if at < blocks}):
+
+            @pl.when(u == at)
+            def _():
+                for when, v in seconds:
+                    if when == at:
+                        item(v, 2, 0)
+
+        gram(u, 0)
         return 0
 
+    def compute_late(u, _):
+        @pl.when(u % 2 == 1)
+        def _():
+            hand_over(u - 1, 1)
+
+        @pl.when((u % 2 == 1) & (u >= 1 + late_lag))
+        def _():
+            second_stage((u - late_lag) // 2, 1, 1)
+
+        gram(u, 1)
+        return 0
+
+    def send_later(c):
+        for w in range(blocks // 2):
+            later_second(w, c)
+
     lax.fori_loop(0, blocks, compute, 0)
 
     for w in range(max(blocks // 2 - lag // 2, 0), blocks // 2):
-        second_stage(w, early)
+        second_stage(w, 0, early)
     for at, v in seconds:
         if at >= blocks:
-            item(v, 2, 0, True)
-
-    def send_later(c, _):
-        for w in range(blocks // 2):
-            later_second(w, c)
-        return 0
-
-    lax.fori_loop(early, chunks, send_later, 0)
+            item(v, 2, 0)
+    for c in range(early, per_pass):
+        send_later(c)
+
+    inside = per_pass >= 4
+    if not inside:
+        lax.fori_loop(0, blocks, compute_late, 0)
+        for w in range(max(blocks // 2 - late_lag // 2, 0), blocks // 2):
+            second_stage(w, 1, per_pass)
 
     turn = phase[...]
     paired = parity_sign(jnp.bitwise_and(px[...], pz[...]))
@@ -356,7 +398,7 @@
     bound_me = jnp.where(mine < blocks // 2, 0, -1)
 
     def finish(c):
-        names = arrive(0, nbits, c, c == 0)
+        names = arrive(0, nbits, c)
         for g in range(group):
             slab = c * group + g
             for r in range(0, own, 8):
@@ -396,15 +438,26 @@
     def step(t, _):
         for s in range(2, nbits):
             c = t - (s - 2)
-            if s == 2:
-                first, live = False, c < chunks
-            else:
-                first, live = c == 0, (c >= 0) & (c < chunks)
-
-            @pl.when(live)
+
+            @pl.when((c >= 0) & (c < chunks))
             def _():
                 for v in range((1 << (nbits - s)) - 1, (1 << (nbits - 1 - s)) - 1, -1):
-                    item(v, s, c, first)
+                    item(v, s, c)
+
+            if s == 2 and inside:
+
+                @pl.when(t < 3)
+                def _():
+                    lax.fori_loop((t - 1) * (blocks // 2), t * (blocks // 2), compute_late, 0)
+
+                @pl.when(t == 3)
+                def _():
+                    for w in range(blocks // 2 - late_lag // 2, blocks // 2):
+                        second_stage(w, 1, 1)
+
+                @pl.when((t >= 3) & (t - 3 < per_pass - 1))
+                def _():
+                    send_later(per_pass + t - 2)
 
         @pl.when((t >= last) & (t - last < chunks))
         def _():
@@ -454,7 +507,14 @@
             mirrored[slabs * q + sub] = came[slabs * q + sub]
 
     def drain(ident, _):
-        whole(0, ident).wait_send()
+        pltpu.make_async_remote_copy(
+            src_ref=part.at[0],
+            dst_ref=land.at[ident],
+            send_sem=send_sem.at[ident],
+            recv_sem=recv_sem.at[0],
+            device_id=coords(partner[0], sizes),
+            device_id_type=MESH,
+        ).wait_send()
         return 0
 
     lax.fori_loop(1, n, drain, 0)
@@ -520,7 +580,7 @@
     vmem = pl.BlockSpec(memory_space=pltpu.VMEM)
     terms = pauli_x.shape[0]
     kept, mirrored, expect = pl.pallas_call(
-        functools.partial(gram_kernel, sizes, float(depth * n), min(EARLY, chunks)),
+        functools.partial(gram_kernel, sizes, float(depth * n), min(EARLY, chunks // 2)),
         out_shape=(
             jax.ShapeDtypeStruct((slabs, own, 2 * block), jnp.float32),
             jax.ShapeDtypeStruct((slots, own, 2 * own), jnp.float32),
@@ -546,7 +606,7 @@
             pltpu.SemaphoreType.DMA((n,)),
             pltpu.SemaphoreType.DMA((n,)),
         ],
-        compiler_params=pltpu.CompilerParams(has_side_effects=True, vmem_limit_bytes=60 << 20),
+        compiler_params=pltpu.CompilerParams(collective_id=0, has_side_effects=True, vmem_limit_bytes=VMEM_LIMIT),
     )(amplitudes, pauli_x[None], pauli_z[None], pauli_phase[None])
     real, imag, expect = pl.pallas_call(
         functools.partial(finish_kernel, sizes),

time: 109 us -> 97.5 us (0.89)
  Pallas kernels: 108 us -> 96.7 us
    pallas_call x1, Pallas kernels: 106 us -> 94.3 us  [on_device(): pl.pallas_call(functools.partial(gram_kernel, sizes, float(depth * n), mi...]
where the time goes in v2:
time: 97.5 us; the launch traced here: 97.3 us
  Pallas kernels  96.7 us (99%)
    pallas_call x1, Pallas kernels, on_device(): pl.pallas_call(functools.partial(gram_kernel, sizes, float(depth * n), mi...  94.3 us
    pallas_call x1, Pallas kernels, on_device(): pl.pallas_call(functools.partial(finish_kernel, sizes), out_shape=(jax.Sh...  2.39 us

profile of v2, /device:TPU:0, one launch (start us, length us, event | category | flops | bytes accessed | tf_op | source)
XLA Modules:
  0.0 97.3 jit_solution(5813234205581160579)
XLA Ops:
  0.6 94.3 %shard_map.67 = (f32[8,64,256]{2,1,0:T(8,128)}, f32[18,64,128]{2,1,0:T(8,128)}, f32[2,200]{1,0:T(2,128)}) custom-call(bf16[2,512,2048]{2,1,0:T(8,128)(2,1)} %amp.1, s32[1,200]{1,0:T(1,128)} %bitcast.3, s32[1,200]{1,0:T(1,128)} %bitcast.4, s32[1,200]{1,0:T(1,128)} %bitcast.5), custom_call_target="tpu_custom_call" | custom-call | tf_op jit(solution)/shard_map/pallas_call | solution.py:582
  94.9 2.4 %shard_map.68 = (f32[64,2048]{1,0:T(8,128)}, f32[64,2048]{1,0:T(8,128)}, f32[2,200]{1,0:T(2,128)}) custom-call(f32[8,64,256]{2,1,0:T(8,128)} %get-tuple-element.6.kept, f32[18,64,128]{2,1,0:T(8,128)} %get-tuple-element.7.mirrored, f32[2,200]{1,0:T(2,128)} %get-tuple-element.8.expected), custom_call_target="tpu_custom_call" | custom-call | tf_op jit(solution)/shard_map/pallas_call | solution.py:611

commit v3 on v2

--- a/solution.py
+++ b/solution.py
@@ -10,6 +10,11 @@
 AXES = ("gx", "gy", "gz")
 LANES = 128
 EARLY = 2
+OFFSETS = (0.0, 0.246, 0.02)
+SPREAD = 0.4
+FINISH_AT = 0.124
+REFLECT_AFTER = 0.145
+GRAMS_AT = (0.5, 0.75, 0.8)
 VMEM_LIMIT = 60 << 20
 MESH = pl.DeviceIdType.MESH
 
@@ -184,39 +189,30 @@
             total = total + land[ident, slab, rows, :]
         return total
 
-    def second_stage(w, which, upto):
+    def join(w, which, upto):
+        for g in range(q):
+            flips = with_low(row_block(2 * w + 1), g)
+            where, ident = place(flips), name(flips)
+            across(where, ident + (1 << stages[0]), which).wait_recv()
+            for slab in range(which * part_slabs, (which + 1) * part_slabs):
+                for r in range(0, own, 8):
+                    rows = pl.ds(r, 8)
+                    part[where, slab, rows, :] = summed(where, [ident + (1 << stages[0])], slab, rows)
+        for c in range(which * per_pass, which * per_pass + upto):
+            send_first(w, c)
+
+    def send_first(w, c):
         for g in range(q):
             flips = with_low(row_block(2 * w + 1), g)
             goes = flips[stages[1]] * (1 - half) + flips[stages[trade]] * half
 
             @pl.when(goes == 1)
             def _():
-                where, ident = place(flips), name(flips)
-                across(where, ident + (1 << stages[0]), which).wait_recv()
-                for slab in range(which * part_slabs, (which + 1) * part_slabs):
-                    for r in range(0, own, 8):
-                        rows = pl.ds(r, 8)
-                        part[where, slab, rows, :] = summed(where, [ident + (1 << stages[0])], slab, rows)
-                for c in range(which * per_pass, which * per_pass + upto):
-                    message(where, ident, partner[1], c).start()
-
-    def later_second(w, c):
-        for g in range(q):
-            flips = with_low(row_block(2 * w + 1), g)
-            goes = flips[stages[1]] * (1 - half) + flips[stages[trade]] * half
-
-            @pl.when(goes == 1)
-            def _():
                 message(place(flips), name(flips), partner[1], c).start()
 
     def arrive(v, upto, c):
-        names = [name(flips_of(v | (1 << (nbits - 1 - t)))) for t in range(upto)]
-
-        @pl.when(c % per_pass == 0)
-        def _():
-            across(0, names[0], c // per_pass).wait_recv()
-
-        for ident in names[1:]:
+        names = [name(flips_of(v | (1 << (nbits - 1 - t)))) for t in range(1, upto)]
+        for ident in names:
             message(0, ident, partner[0], c).wait_recv()
         return names
 
@@ -292,7 +288,7 @@
 
         @pl.when((u % 2 == 1) & (u >= 1 + lag))
         def _():
-            second_stage((u - lag) // 2, 0, early)
+            join((u - lag) // 2, 0, early)
 
         for at in sorted({at for at, _ in seconds if at < blocks}):
 
@@ -312,19 +308,19 @@
 
         @pl.when((u % 2 == 1) & (u >= 1 + late_lag))
         def _():
-            second_stage((u - late_lag) // 2, 1, 1)
+            join((u - late_lag) // 2, 1, 1)
 
         gram(u, 1)
         return 0
 
     def send_later(c):
         for w in range(blocks // 2):
-            later_second(w, c)
+            send_first(w, c)
 
     lax.fori_loop(0, blocks, compute, 0)
 
     for w in range(max(blocks // 2 - lag // 2, 0), blocks // 2):
-        second_stage(w, 0, early)
+        join(w, 0, early)
     for at, v in seconds:
         if at >= blocks:
             item(v, 2, 0)
@@ -335,7 +331,7 @@
     if not inside:
         lax.fori_loop(0, blocks, compute_late, 0)
         for w in range(max(blocks // 2 - late_lag // 2, 0), blocks // 2):
-            second_stage(w, 1, per_pass)
+            join(w, 1, per_pass)
 
     turn = phase[...]
     paired = parity_sign(jnp.bitwise_and(px[...], pz[...]))
@@ -408,24 +404,11 @@
 
             @pl.when(slab < slabs - 1)
             def _():
-                for sub in range(q):
-                    mirror(slab + 1, sub, slab, slab).start()
                 pick(kept[slab, :, :block], kept[slab, :, block:], slab + 1)
 
         @pl.when(c == chunks - 1)
         def _():
             slab = slabs - 1
-            for sub in range(q):
-                mirror(slabs, sub, slab, slab).start()
-
-                @pl.when(sub != sub_me)
-                def _():
-                    mirror(0, sub, slab, slabs).start()
-
-                @pl.when(sub == sub_me)
-                def _():
-                    mirrored[slabs * q + sub] = turned[slab, sub * own : (sub + 1) * own]
-
             near = kept[slab, :, :block]
             upper = jnp.where(local_row < lane, near, jnp.where(local_row == lane, 0.5 * near, 0.0))
             pick(upper, jnp.where(local_row > lane, near, 0.0), 0)
@@ -433,35 +416,81 @@
             holds = local_row - lane <= bound_me
             pick(jnp.where(holds, far, 0.0), jnp.where(holds, 0.0, far), slabs)
 
-    last = nbits - 2
+    def reflect(c):
+        for g in range(group):
+            slab = c * group + g
+            for sub in range(q):
+                mirror(slab + 1, sub, slab, slab).start()
+
+        @pl.when(c == chunks - 1)
+        def _():
+            slab = slabs - 1
+            for sub in range(q):
+
+                @pl.when(sub != sub_me)
+                def _():
+                    mirror(0, sub, slab, slabs).start()
+
+                @pl.when(sub == sub_me)
+                def _():
+                    mirrored[slabs * q + sub] = turned[slab, sub * own : (sub + 1) * own]
+
+    def late_grams(t, part_of):
+        if not inside:
+            return
+        count = blocks // 4
+
+        @pl.when(t < 3)
+        def _():
+            begin = (2 * (t - 1) + part_of) * count
+            lax.fori_loop(begin, begin + count, compute_late, 0)
+
+        @pl.when(t == 3)
+        def _():
+            begin = blocks // 2 - late_lag // 2 + part_of * (late_lag // 4)
+            for w in range(begin, begin + late_lag // 4):
+                join(w, 1, 1)
+
+    def late_sends(t):
+        if not inside:
+            return
+
+        @pl.when((t >= 3) & (t - 3 < per_pass - 1))
+        def _():
+            send_later(per_pass + t - 2)
+
+    def body():
+        out = []
+
+        def add(at, lowest, action):
+            out.append((at - int(at), int(at), lowest, action))
+
+        for s in range(2, nbits):
+            at = OFFSETS[0] if s == 2 else s - 2 + (OFFSETS[2] if s == nbits - 1 else OFFSETS[1])
+            count = 1 << (nbits - 1 - s)
+            for i in range(count):
+                v = 2 * count - 1 - i
+                add(at + SPREAD * i / count, 1 if s == 2 else 0, functools.partial(item, v, s))
+        add(nbits + FINISH_AT, 0, finish)
+        add(nbits + FINISH_AT + REFLECT_AFTER, 0, reflect)
+        for part_of in range(2):
+            out.append((GRAMS_AT[part_of], None, 0, functools.partial(lambda which, t: late_grams(t, which), part_of)))
+        out.append((GRAMS_AT[2], None, 0, late_sends))
+        return sorted(out, key=lambda entry: entry[0])
+
+    turn_body = body()
+    last = max(delay for _, delay, _, _ in turn_body if delay is not None)
 
     def step(t, _):
-        for s in range(2, nbits):
-            c = t - (s - 2)
-
-            @pl.when((c >= 0) & (c < chunks))
+        for _, delay, lowest, action in turn_body:
+            if delay is None:
+                action(t)
+                continue
+            c = t - delay
+
+            @pl.when((c >= lowest) & (c < chunks))
             def _():
-                for v in range((1 << (nbits - s)) - 1, (1 << (nbits - 1 - s)) - 1, -1):
-                    item(v, s, c)
-
-            if s == 2 and inside:
-
-                @pl.when(t < 3)
-                def _():
-                    lax.fori_loop((t - 1) * (blocks // 2), t * (blocks // 2), compute_late, 0)
-
-                @pl.when(t == 3)
-                def _():
-                    for w in range(blocks // 2 - late_lag // 2, blocks // 2):
-                        second_stage(w, 1, 1)
-
-                @pl.when((t >= 3) & (t - 3 < per_pass - 1))
-                def _():
-                    send_later(per_pass + t - 2)
-
-        @pl.when((t >= last) & (t - last < chunks))
-        def _():
-            finish(t - last)
+                action(c)
 
         return 0
 

time: 97.5 us -> 95.5 us (0.979)
  Pallas kernels: 96.7 us -> 94.7 us
    pallas_call x1, Pallas kernels: 94.3 us -> 92.3 us  [on_device(): pl.pallas_call(functools.partial(gram_kernel, sizes, float(depth * n), mi...]
where the time goes in v3:
time: 95.5 us; the launch traced here: 95.3 us
  Pallas kernels  94.7 us (99%)
    pallas_call x1, Pallas kernels, on_device(): pl.pallas_call(functools.partial(gram_kernel, sizes, float(depth * n), mi...  92.3 us
    pallas_call x1, Pallas kernels, on_device(): pl.pallas_call(functools.partial(finish_kernel, sizes), out_shape=(jax.Sh...  2.39 us

profile of v3, /device:TPU:0, one launch (start us, length us, event | category | flops | bytes accessed | tf_op | source)
XLA Modules:
  0.0 95.3 jit_solution(7961691918755497794)
XLA Ops:
  0.6 92.3 %shard_map.67 = (f32[8,64,256]{2,1,0:T(8,128)}, f32[18,64,128]{2,1,0:T(8,128)}, f32[2,200]{1,0:T(2,128)}) custom-call(bf16[2,512,2048]{2,1,0:T(8,128)(2,1)} %amp.1, s32[1,200]{1,0:T(1,128)} %bitcast.3, s32[1,200]{1,0:T(1,128)} %bitcast.4, s32[1,200]{1,0:T(1,128)} %bitcast.5), custom_call_target="tpu_custom_call" | custom-call | tf_op jit(solution)/shard_map/pallas_call | solution.py:611
  93.0 2.4 %shard_map.68 = (f32[64,2048]{1,0:T(8,128)}, f32[64,2048]{1,0:T(8,128)}, f32[2,200]{1,0:T(2,128)}) custom-call(f32[8,64,256]{2,1,0:T(8,128)} %get-tuple-element.6.kept, f32[18,64,128]{2,1,0:T(8,128)} %get-tuple-element.7.mirrored, f32[2,200]{1,0:T(2,128)} %get-tuple-element.8.expected), custom_call_target="tpu_custom_call" | custom-call | tf_op jit(solution)/shard_map/pallas_call | solution.py:640

commit v4 on v3

--- a/solution.py
+++ b/solution.py
@@ -13,9 +13,9 @@
 OFFSETS = (0.0, 0.246, 0.02)
 SPREAD = 0.4
 FINISH_AT = 0.124
-REFLECT_AFTER = 0.145
-GRAMS_AT = (0.5, 0.75, 0.8)
-VMEM_LIMIT = 60 << 20
+REFLECT_AFTER = 1.0
+GRAMS_AT = (0.28, 0.35, 0.5)
+VMEM_LIMIT = 52 << 20
 MESH = pl.DeviceIdType.MESH
 
 
@@ -88,8 +88,8 @@
 
 
 def gram_kernel(
-    sizes, total_cols, early, amp, px, pz, phase, kept, mirrored, expect,
-    ext, part, land, turned, came, spread, tally, outbox, inbox, load_sem, send_sem, recv_sem, msend, mrecv, esend, erecv,
+    sizes, total_cols, early, amp, px_in, pz_in, phase_in, kept, mirrored, expect,
+    ext, px, pz, phase, part, land, turned, came, spread, tally, outbox, inbox, load_sem, mask_sem, send_sem, recv_sem, msend, mrecv, esend, erecv,
 ):
     n = sizes[0] * sizes[1] * sizes[2]
     nbits = log2(n)
@@ -148,6 +148,12 @@
         pl.semaphore_signal(barrier, inc=1, device_id=coords(other, sizes), device_id_type=MESH)
     for copy in loads():
         copy.start()
+    masks = [
+        pltpu.make_async_copy(source, target, mask_sem.at[i])
+        for i, (source, target) in enumerate(((px_in, px), (pz_in, pz), (phase_in, phase)))
+    ]
+    for copy in masks:
+        copy.start()
     lowbits = log2(q)
     high = row_order(sizes, q)
 
@@ -333,6 +339,8 @@
         for w in range(max(blocks // 2 - late_lag // 2, 0), blocks // 2):
             join(w, 1, per_pass)
 
+    for copy in masks:
+        copy.wait()
     turn = phase[...]
     paired = parity_sign(jnp.bitwise_and(px[...], pz[...]))
     wanted = jnp.bitwise_xor(px[...], base)
@@ -615,10 +623,11 @@
             jax.ShapeDtypeStruct((slots, own, 2 * own), jnp.float32),
             jax.ShapeDtypeStruct((2, terms), jnp.float32),
         ),
-        in_specs=[pl.BlockSpec(memory_space=pl.ANY), vmem, vmem, vmem],
+        in_specs=[pl.BlockSpec(memory_space=pltpu.HBM)] * 4,
         out_specs=(vmem,) * 3,
         scratch_shapes=[
             pltpu.VMEM((2 * depth, order + width - block), jnp.bfloat16),
+            *[pltpu.VMEM((1, terms), jnp.int32)] * 3,
             pltpu.VMEM((n, slabs, own, 2 * block), jnp.float32),
             pltpu.VMEM((n, slabs, own, 2 * block), jnp.float32),
             pltpu.VMEM((slabs, block, 2 * own), jnp.float32),
@@ -628,6 +637,7 @@
             pltpu.VMEM((2, terms), jnp.float32),
             pltpu.VMEM((n, 2, terms), jnp.float32),
             pltpu.SemaphoreType.DMA((4,)),
+            pltpu.SemaphoreType.DMA((3,)),
             pltpu.SemaphoreType.DMA((n,)),
             pltpu.SemaphoreType.DMA((n * chunks,)),
             pltpu.SemaphoreType.DMA((slots,)),
@@ -636,7 +646,7 @@
             pltpu.SemaphoreType.DMA((n,)),
         ],
         compiler_params=pltpu.CompilerParams(collective_id=0, has_side_effects=True, vmem_limit_bytes=VMEM_LIMIT),
-    )(amplitudes, pauli_x[None], pauli_z[None], pauli_phase[None])
+    )(amplitudes, *[pltpu.with_memory_space_constraint(m[None], pltpu.HBM) for m in (pauli_x, pauli_z, pauli_phase)])
     real, imag, expect = pl.pallas_call(
         functools.partial(finish_kernel, sizes),
         out_shape=(
@@ -646,6 +656,7 @@
         ),
         in_specs=[vmem] * 3,
         out_specs=(vmem,) * 3,
+        compiler_params=pltpu.CompilerParams(vmem_limit_bytes=8 << 20),
     )(kept, mirrored, expect)
     return real, imag, expect
 

time: 95.5 us -> 91.8 us (0.961)
  Pallas kernels: 94.7 us -> 91 us
    pallas_call x1, Pallas kernels: 92.3 us -> 89.9 us  [on_device(): pl.pallas_call(functools.partial(gram_kernel, sizes, float(depth * n), mi...]
    pallas_call x1, Pallas kernels: 2.39 us -> 1.17 us  [on_device(): pl.pallas_call(functools.partial(finish_kernel, sizes), out_shape=(jax.Sh...]
where the time goes in v4:
time: 91.8 us; the launch traced here: 91.7 us
  Pallas kernels  91 us (99%)
    pallas_call x1, Pallas kernels, on_device(): pl.pallas_call(functools.partial(gram_kernel, sizes, float(depth * n), mi...  89.9 us

profile of v4, /device:TPU:0, one launch (start us, length us, event | category | flops | bytes accessed | tf_op | source)
XLA Modules:
  0.0 91.7 jit_solution(2613263514351207481)
XLA Ops:
  0.6 89.9 %shard_map.67 = (f32[8,64,256]{2,1,0:T(8,128)S(1)}, f32[18,64,128]{2,1,0:T(8,128)S(1)}, f32[2,200]{1,0:T(2,128)S(1)}) custom-call(bf16[2,512,2048]{2,1,0:T(8,128)(2,1)} %amp.1, s32[1,200]{1,0:T(1,128)} %bitcast.3, s32[1,200]{1,0:T(1,128)} %bitcast.4, s32[1,200]{1,0:T(1,128)} %bitcast.5), custom_call_target="tpu_custom_call" | custom-call | tf_op jit(solution)/shard_map/pallas_call | solution.py:619
  90.5 1.2 %shard_map.68 = (f32[64,2048]{1,0:T(8,128)}, f32[64,2048]{1,0:T(8,128)}, f32[2,200]{1,0:T(2,128)}) custom-call(f32[8,64,256]{2,1,0:T(8,128)S(1)} %get-tuple-element.6.kept, f32[18,64,128]{2,1,0:T(8,128)S(1)} %get-tuple-element.7.mirrored, f32[2,200]{1,0:T(2,128)S(1)} %get-tuple-element.8.expected), custom_call_target="tpu_custom_call" | custom-call | tf_op jit(solution)/shard_map/pallas_call | solution.py:650

commit v5 on v4

--- a/solution.py
+++ b/solution.py
@@ -112,6 +112,8 @@
     half = bits[stages[0]]
     lag, late_lag, flight = 4, blocks // 2, 6
 
+    wrap = part_slabs * block
+
     def loads():
         out = []
         for part_index in range(2):
@@ -119,13 +121,20 @@
             out.append(pltpu.make_async_copy(amp.at[part_index], ext.at[rows, pl.ds(0, order)], load_sem.at[2 * part_index]))
             out.append(
                 pltpu.make_async_copy(
-                    amp.at[part_index, :, pl.ds(0, width - block)],
-                    ext.at[rows, pl.ds(order, width - block)],
+                    amp.at[part_index, :, pl.ds(0, wrap)],
+                    ext.at[rows, pl.ds(order, wrap)],
                     load_sem.at[2 * part_index + 1],
                 )
             )
+        for part_index in range(2):
+            out.append(
+                pltpu.make_async_copy(
+                    amp.at[part_index, :, pl.ds(wrap, width - block - wrap)],
+                    ext.at[pl.ds(part_index * depth, depth), pl.ds(order + wrap, width - block - wrap)],
+                    load_sem.at[4 + part_index],
+                )
+            )
         return out
-
 
     def flips_of(v):
         by_stage = [(v >> (nbits - 1 - s)) & 1 for s in range(nbits)]
@@ -238,7 +247,7 @@
     sub_me = me % q
     base = me * own
 
-    for copy in loads():
+    for copy in loads()[:4]:
         copy.wait()
 
     row_in = lax.broadcasted_iota(jnp.int32, (block, block), 0)
@@ -324,6 +333,8 @@
             send_first(w, c)
 
     lax.fori_loop(0, blocks, compute, 0)
+    for copy in loads()[4:]:
+        copy.wait()
 
     for w in range(max(blocks // 2 - lag // 2, 0), blocks // 2):
         join(w, 0, early)
@@ -636,7 +647,7 @@
             pltpu.VMEM((1, terms), jnp.float32),
             pltpu.VMEM((2, terms), jnp.float32),
             pltpu.VMEM((n, 2, terms), jnp.float32),
-            pltpu.SemaphoreType.DMA((4,)),
+            pltpu.SemaphoreType.DMA((6,)),
             pltpu.SemaphoreType.DMA((3,)),
             pltpu.SemaphoreType.DMA((n,)),
             pltpu.SemaphoreType.DMA((n * chunks,)),

time: 91.8 us -> 91.5 us (level)
  no operation moved by 1% of the time
where the time goes in v5:
time: 91.5 us; the launch traced here: 91.3 us
  Pallas kernels  90.7 us (99%)
    pallas_call x1, Pallas kernels, on_device(): pl.pallas_call(functools.partial(gram_kernel, sizes, float(depth * n), mi...  89.5 us

profile of v5, /device:TPU:0, one launch (start us, length us, event | category | flops | bytes accessed | tf_op | source)
XLA Modules:
  0.0 91.3 jit_solution(3734773155944636980)
XLA Ops:
  0.6 89.5 %shard_map.67 = (f32[8,64,256]{2,1,0:T(8,128)S(1)}, f32[18,64,128]{2,1,0:T(8,128)S(1)}, f32[2,200]{1,0:T(2,128)S(1)}) custom-call(bf16[2,512,2048]{2,1,0:T(8,128)(2,1)} %amp.1, s32[1,200]{1,0:T(1,128)} %bitcast.3, s32[1,200]{1,0:T(1,128)} %bitcast.4, s32[1,200]{1,0:T(1,128)} %bitcast.5), custom_call_target="tpu_custom_call" | custom-call | tf_op jit(solution)/shard_map/pallas_call | solution.py:630
  90.2 1.2 %shard_map.68 = (f32[64,2048]{1,0:T(8,128)}, f32[64,2048]{1,0:T(8,128)}, f32[2,200]{1,0:T(2,128)}) custom-call(f32[8,64,256]{2,1,0:T(8,128)S(1)} %get-tuple-element.6.kept, f32[18,64,128]{2,1,0:T(8,128)S(1)} %get-tuple-element.7.mirrored, f32[2,200]{1,0:T(2,128)S(1)} %get-tuple-element.8.expected), custom_call_target="tpu_custom_call" | custom-call | tf_op jit(solution)/shard_map/pallas_call | solution.py:661

commit v6 on v5

--- a/solution.py
+++ b/solution.py
@@ -10,7 +10,7 @@
 AXES = ("gx", "gy", "gz")
 LANES = 128
 EARLY = 2
-OFFSETS = (0.0, 0.246, 0.02)
+OFFSETS = (0.0, 0.12, 0.02)
 SPREAD = 0.4
 FINISH_AT = 0.124
 REFLECT_AFTER = 1.0

time: 91.5 us -> 91.5 us (level)
  no operation moved by 1% of the time
where the time goes in v6:
time: 91.5 us; the launch traced here: 91.3 us
  Pallas kernels  90.7 us (99%)
    pallas_call x1, Pallas kernels, on_device(): pl.pallas_call(functools.partial(gram_kernel, sizes, float(depth * n), mi...  89.5 us

profile of v6, /device:TPU:0, one launch (start us, length us, event | category | flops | bytes accessed | tf_op | source)
XLA Modules:
  0.0 91.3 jit_solution(5226386924633584235)
XLA Ops:
  0.6 89.5 %shard_map.67 = (f32[8,64,256]{2,1,0:T(8,128)S(1)}, f32[18,64,128]{2,1,0:T(8,128)S(1)}, f32[2,200]{1,0:T(2,128)S(1)}) custom-call(bf16[2,512,2048]{2,1,0:T(8,128)(2,1)} %amp.1, s32[1,200]{1,0:T(1,128)} %bitcast.3, s32[1,200]{1,0:T(1,128)} %bitcast.4, s32[1,200]{1,0:T(1,128)} %bitcast.5), custom_call_target="tpu_custom_call" | custom-call | tf_op jit(solution)/shard_map/pallas_call | solution.py:630
  90.2 1.2 %shard_map.68 = (f32[64,2048]{1,0:T(8,128)}, f32[64,2048]{1,0:T(8,128)}, f32[2,200]{1,0:T(2,128)}) custom-call(f32[8,64,256]{2,1,0:T(8,128)S(1)} %get-tuple-element.6.kept, f32[18,64,128]{2,1,0:T(8,128)S(1)} %get-tuple-element.7.mirrored, f32[2,200]{1,0:T(2,128)S(1)} %get-tuple-element.8.expected), custom_call_target="tpu_custom_call" | custom-call | tf_op jit(solution)/shard_map/pallas_call | solution.py:661
